TPU v7x, 512 devices: a whole 4x8x8 slice. The times are simulated.
512 devices in a mesh: chip: 32 (over x_hi, y, core), line: 16 (over z, x_lo).
Axes of the slice: x: 4 (x_hi: 2, x_lo: 2; x = x_hi * 2 + x_lo), y: 8, z: 8, core: 2. Of those that a mesh axis runs over, the one named last changes fastest.
Arguments:
- echoes: bfloat16 [32, 2, 4096, 4096], P('chip', None, 'line'), may hold values from -6 to 6
- range_filter: float32 [2, 4096], replicated, may hold values from -6 to 6
- rcmc_weights: float32 [8, 4096], replicated, may hold values from -3 to 3
- fm_rate: float32 [32, 384], P('chip', 'line'), may hold values from 256 to 2048
- rcmc_shift: int32 [32, 384], P('chip', 'line'), may hold values from 0 to 12, as said below
- seam_width: int32 [32], P('chip'), may hold values from 64 to 128, as said below
- seam_link: int32 [32], P('chip'), may hold values from 0 to 1
Outputs:
- image: bfloat16 [32, 2, 384, 4096], P('chip', None, 'line')
Inputs may be any that keep to these rules, and one draw needn't show every extreme that they name: `rcmc_shift`: every draw has some entry equal to 12. `seam_width`: every draw has some chip with the width 128.
All inputs are finite; a program needn't handle non-finite values.
Results may differ from a plain program's by a relative error of at most 0.0011.
Values sent between devices are 32-bit elements; how exact they have to be, the bound alone decides.
A program may use at most 64 MiB of HBM per device.

v0:
```python
import math

import jax
import jax.numpy as jnp
import numpy as np
from jax import lax
from jax.experimental import pallas as pl
from jax.experimental.pallas import tpu as pltpu
from jax.sharding import PartitionSpec as P

F32 = jnp.float32
BF16 = jnp.bfloat16
AZ = 4096
RKEEP = 384
TAPS = 8
OVL = 128
LINES = 16
ROWS = RKEEP // LINES
NEED = 44
SLOT = 104
HIGHEST = lax.Precision.HIGHEST
MESH = pl.DeviceIdType.MESH


def place(comp, i):
    if i < 16:
        return comp * 16 + i
    if i < 20:
        return 32 + comp * 4 + i - 16
    return 40 + comp * 4 + i - 20


def split(value):
    high = value.astype(BF16)
    return high, (value - high.astype(F32)).astype(BF16)


def angles(rows, columns, length, sign):
    product = np.outer(np.asarray(rows, np.int64), np.asarray(columns, np.int64)) % length
    theta = sign * 2.0 * np.pi / length * product
    return np.cos(theta), np.sin(theta)


def split_table(table, axis):
    import ml_dtypes

    high = table.astype(np.float32).astype(ml_dtypes.bfloat16)
    low = (table - high.astype(np.float64)).astype(np.float32).astype(ml_dtypes.bfloat16)
    return np.concatenate([high, high, low], axis=axis)


def tables():
    n32, n128 = np.arange(32), np.arange(128)
    c, s = angles(n32, n32, 32, -1)
    first = np.block([[c, -s], [s, c]])
    filter_turn = np.stack(angles(n32, n128, 4096, -1))
    shift = (4 * n32[None, :] - np.arange(4)[:, None]).reshape(-1)
    c, s = angles(shift, n128, 128, 1)
    second = np.block([[c, -s], [s, c]]) / 4096.0
    c, s = angles(n32, n32, 32, -1)
    forward32 = np.block([[c, -s], [s, c]])
    turn = np.stack(angles(n32, n128, 4096, -1))
    c, s = angles(n128, n128, 128, -1)
    forward128 = np.block([[c, s], [-s, c]])
    c, s = angles(n128, n128, 128, 1)
    inverse128 = np.block([[c, s], [-s, c]])
    c, s = angles(n32, n32, 32, 1)
    inverse32 = np.block([[c, -s], [s, c]]) / 4096.0
    f32 = lambda t: t.astype(np.float32)
    return (
        f32(first),
        f32(filter_turn),
        f32(second),
        split_table(forward32, 1),
        f32(turn),
        split_table(forward128, 0),
        split_table(inverse128, 0),
        split_table(inverse32, 1),
    )


def mm(a, b, precision=None):
    return lax.dot_general(
        a, b, (((1,), (0,)), ((), ())), precision=precision, preferred_element_type=F32
    )


def mm_nt(a, b, precision=None):
    return lax.dot_general(
        a, b, (((1,), (1,)), ((), ())), precision=precision, preferred_element_type=F32
    )


def turned(real, imag, c, s):
    return real * c - imag * s, real * s + imag * c


def kernel(
    chips,
    echo_hbm,
    filter_ref,
    weight_ref,
    rate_ref,
    shift_ref,
    width_ref,
    link_ref,
    first_ref,
    fturn_ref,
    second_ref,
    fwd32_ref,
    turn_ref,
    fwd128_ref,
    inv128_ref,
    inv32_ref,
    out_ref,
    echo,
    spectrum,
    pulse,
    band,
    acc,
    piece,
    recv,
    mid_hi,
    mid_lo,
    ext,
    cosine,
    sine,
    foc_hi,
    foc_lo,
    back,
    img,
    tail,
    tail_in,
    esend,
    erecv,
    load_sem,
    send_sem,
    recv_sem,
    fsend_sem,
    frecv_sem,
    tail_sem,
    esend_sem,
    erecv_sem,
):
    me = lax.axis_index("line")
    chip = lax.axis_index("chip")
    following = lax.rem(chip + 1, chips)
    preceding = lax.rem(chip + chips - 1, chips)
    below = lax.rem(me + LINES - 1, LINES)
    barrier = pltpu.get_barrier_semaphore()

    @pl.loop(1, LINES)
    def _(k):
        pl.semaphore_signal(
            barrier, inc=1, device_id={"line": lax.rem(me + k, LINES)}, device_id_type=MESH
        )

    pl.semaphore_signal(barrier, inc=1, device_id={"chip": following}, device_id_type=MESH)
    pl.semaphore_signal(barrier, inc=1, device_id={"chip": preceding}, device_id_type=MESH)

    def load(c):
        return pltpu.make_async_copy(
            echo_hbm.at[0, :, pl.ds(128 * c, 128), :],
            echo.at[:, pl.ds(128 * c, 128), :],
            load_sem.at[c],
        )

    load(0).start()
    load(1).start()

    for comp in range(2):
        for a in range(32):
            spectrum[pl.ds(comp * 32 + a, 1), :] = filter_ref[comp : comp + 1, 128 * a : 128 * a + 128]
    y = mm(first_ref[...], spectrum[...], HIGHEST)
    yr, yi = turned(y[:32], y[32:], fturn_ref[0], fturn_ref[1])
    y = mm_nt(second_ref[...], jnp.concatenate([yr, yi], axis=1), HIGHEST)
    for comp in range(2):
        rows = jnp.concatenate(
            [y[128 * comp + 32 * u : 128 * comp + 32 * u + 32] for u in range(4)], axis=1
        )
        pulse[pl.ds(40 * comp, 32), :] = rows
        pulse[pl.ds(40 * comp + 32, 8), :] = rows[:8]

    keep = lax.broadcasted_iota(jnp.int32, (128, 128), 1) >= lax.broadcasted_iota(
        jnp.int32, (128, 128), 0
    )

    def slanted(comp, m):
        row = pulse[pl.ds(40 * comp + m, 1), :]
        return pltpu.roll(
            jnp.broadcast_to(row, (128, 128)), 0, axis=1, stride=1, stride_axis=0
        )

    def build(m, carry):
        new = []
        at = pl.multiple_of(128 * m, 128)
        for comp in range(2):
            ahead = slanted(comp, m + 1)
            high, low = split(jnp.where(keep, carry[comp], ahead))
            band[2 * comp, pl.ds(at, 128), :] = high
            band[2 * comp + 1, pl.ds(at, 128), :] = low
            new.append(ahead)
        return tuple(new)

    lax.fori_loop(0, 34, build, (slanted(0, 0), slanted(1, 0)))

    def multiply(c):
        acc[...] = jnp.zeros_like(acc)

        @pl.loop(0, 16)
        def _(t):
            s = pl.multiple_of(256 * t, 256)
            at0 = pl.multiple_of(128 * lax.rem(32 - 2 * t, 32), 128)
            at1 = pl.multiple_of(128 * (31 - 2 * t), 128)
            xr = echo[0, 128 * c : 128 * c + 128, pl.ds(s, 256)]
            xi = echo[1, 128 * c : 128 * c + 128, pl.ds(s, 256)]
            right = jnp.concatenate(
                [
                    jnp.concatenate([xr, xr, -xi, -xi], axis=1),
                    jnp.concatenate([xi, xi, xr, xr], axis=1),
                ],
                axis=0,
            )
            left = jnp.concatenate(
                [band[part, pl.ds(at, RKEEP), :] for part in range(4) for at in (at0, at1)],
                axis=1,
            )
            acc[...] += mm_nt(left, right)

        for g in range(LINES):
            ramp = lax.broadcasted_iota(jnp.int32, (ROWS, 1), 0) + ROWS * g
            gain = 1.0 + 2.0 * ramp.astype(F32) / RKEEP
            for comp in range(2):
                v = acc[ROWS * g : ROWS * g + ROWS, 128 * comp : 128 * comp + 128] * gain
                base = 48 * g
                piece[c, base + 16 * comp : base + 16 * comp + 16, :] = v[:16]
                piece[c, base + 32 + 4 * comp : base + 36 + 4 * comp, :] = v[16:20]
                piece[c, base + 40 + 4 * comp : base + 44 + 4 * comp, :] = v[20:]

    def direct(c, k):
        to = lax.rem(me + k, LINES)
        return pltpu.make_async_remote_copy(
            src_ref=piece.at[c, pl.ds(pl.multiple_of(48 * to, 8), 48), :],
            dst_ref=recv.at[pl.ds(pl.multiple_of((2 * me + c) * SLOT, 8), 48), :],
            send_sem=send_sem.at[c, k],
            recv_sem=recv_sem.at[c, k],
            device_id={"line": to},
            device_id_type=MESH,
        )

    def onward(c, k):
        source = lax.rem(me + LINES - k, LINES)
        slot = (2 * source + c) * SLOT
        return pltpu.make_async_remote_copy(
            src_ref=recv.at[pl.ds(pl.multiple_of(slot, 8), 40), :],
            dst_ref=recv.at[pl.ds(pl.multiple_of(slot + 48, 8), 40), :],
            send_sem=fsend_sem.at[c, k],
            recv_sem=frecv_sem.at[c, k],
            device_id={"line": below},
            device_id_type=MESH,
        )

    for c in range(2):
        load(c).wait()
        multiply(c)
        if c == 0:
            pl.semaphore_wait(barrier, LINES + 1)

        @pl.loop(1, LINES)
        def _(k, c=c):
            direct(c, k).start()

        recv[pl.ds(pl.multiple_of((2 * me + c) * SLOT, 8), 48), :] = piece[
            c, pl.ds(pl.multiple_of(48 * me, 8), 48), :
        ]
        onward(c, 0).start()

    index = lax.broadcasted_iota(jnp.int32, (32, 128), 0) + 32 * lax.broadcasted_iota(
        jnp.int32, (32, 128), 1
    )
    frequency = jnp.where(index < AZ // 2, index, index - AZ).astype(F32) / AZ
    squared = frequency * frequency

    @pl.loop(0, ROWS)
    def _(r):
        turns = rate_ref[0, r] * squared
        turns = turns - 2.0 * jnp.round(turns * 0.5)
        cosine[r] = jnp.cos(math.pi * turns)
        sine[r] = jnp.sin(math.pi * turns)

    for c in range(2):

        @pl.loop(1, LINES)
        def _(k, c=c):
            direct(c, k).wait_recv()
            onward(c, k).start()

    for c in range(2):

        @pl.loop(0, LINES)
        def _(k, c=c):
            onward(c, k).wait_recv()

    tc, ts = turn_ref[0], turn_ref[1]
    last = me == LINES - 1

    def column(i):
        def part(comp):
            at = place(comp, i) if i < ROWS else 48 + place(comp, i - ROWS)
            return recv[pl.ds(at, 32, stride=SLOT), :]

        v = jnp.concatenate([part(0), part(1)], axis=0)
        return v if i < ROWS else jnp.where(last, 0.0, v)

    for i in range(0, NEED, 2):
        high, low = split(jnp.concatenate([column(i), column(i + 1)], axis=1))
        y = mm(fwd32_ref[...], jnp.concatenate([high, low, high], axis=0))
        for j in range(2):
            yr, yi = turned(y[:32, 128 * j : 128 * j + 128], y[32:, 128 * j : 128 * j + 128], tc, ts)
            high, low = split(jnp.concatenate([yr, yi], axis=1))
            mid_hi[32 * (i + j) : 32 * (i + j) + 32, :] = high
            mid_lo[32 * (i + j) : 32 * (i + j) + 32, :] = low

    @pl.loop(0, 4)
    def _(j):
        at = pl.multiple_of(352 * j, 32)
        high, low = mid_hi[pl.ds(at, 352), :], mid_lo[pl.ds(at, 352), :]
        y = mm(jnp.concatenate([high, low, high], axis=1), fwd128_ref[...])
        ext[pl.ds(11 * j, 11)] = y.reshape(11, 32, 256)

    @pl.loop(0, ROWS)
    def _(r):
        at = r + shift_ref[0, r]
        real = jnp.zeros((32, 128), F32)
        imag = jnp.zeros((32, 128), F32)
        for t in range(TAPS):
            w = weight_ref[t]
            row = ext[at + t]
            real += w * row[:, :128]
            imag += w * row[:, 128:]
        fr, fi = turned(real, imag, cosine[r], -sine[r])
        high, low = split(jnp.concatenate([fr, fi], axis=1))
        foc_hi[pl.ds(pl.multiple_of(32 * r, 32), 32), :] = high
        foc_lo[pl.ds(pl.multiple_of(32 * r, 32), 32), :] = low

    @pl.loop(0, 3)
    def _(j):
        at = pl.multiple_of(256 * j, 256)
        high, low = foc_hi[pl.ds(at, 256), :], foc_lo[pl.ds(at, 256), :]
        back[pl.ds(at, 256), :] = mm(jnp.concatenate([high, low, high], axis=1), inv128_ref[...])

    for i in range(0, ROWS, 2):
        both = []
        for j in range(2):
            v = back[32 * (i + j) : 32 * (i + j) + 32, :]
            vr, vi = turned(v[:, :128], v[:, 128:], tc, -ts)
            both.append(jnp.concatenate([vr, vi], axis=0))
        high, low = split(jnp.concatenate(both, axis=1))
        y = mm(inv32_ref[...], jnp.concatenate([high, low, high], axis=0))
        for j in range(2):
            img[64 * (i + j) : 64 * (i + j) + 64, :] = y[:, 128 * j : 128 * j + 128]

    for comp in range(2):
        tail[ROWS * comp : ROWS * comp + ROWS, :] = img[pl.ds(32 * comp + 31, ROWS, stride=64), :]
    handed = pltpu.make_async_remote_copy(
        src_ref=tail,
        dst_ref=tail_in,
        send_sem=tail_sem.at[0],
        recv_sem=tail_sem.at[1],
        device_id={"chip": following},
        device_id_type=MESH,
    )
    handed.start()

    rest = (lax.broadcasted_iota(jnp.int32, (8, 128), 0) > 0).astype(F32)

    def gather(r, total):
        v = img[pl.ds(pl.multiple_of(64 * r, 64), 64), :]
        v = v * v
        for j in range(8):
            part = v[8 * j : 8 * j + 8]
            total = total + (part * rest if j % 4 == 0 else part)
        return total

    energy = lax.fori_loop(0, ROWS, gather, jnp.zeros((8, 128), F32))

    handed.wait()
    width = width_ref[0]
    lane = lax.broadcasted_iota(jnp.int32, (1, 128), 1)
    ramp = (lane.astype(F32) + 0.5) / width.astype(F32)
    linked = (link_ref[0] == 1).astype(jnp.int32)
    inside = lane < width * linked
    earlier = jnp.where(chip == 0, 0.0, tail_in[...])
    previous = pltpu.roll(earlier, lax.rem(width, OVL), axis=1)
    for comp in range(2):
        head = img[pl.ds(32 * comp, ROWS, stride=64), :]
        before = previous[ROWS * comp : ROWS * comp + ROWS]
        mixed = jnp.where(inside, (1.0 - ramp) * before + ramp * head, head)
        img[pl.ds(32 * comp, ROWS, stride=64), :] = mixed
        mixed = mixed * mixed
        energy = energy + mixed[:8] + mixed[8:16] + mixed[16:]
    esend[...] = energy

    def share(k):
        return pltpu.make_async_remote_copy(
            src_ref=esend,
            dst_ref=erecv.at[k],
            send_sem=esend_sem.at[k],
            recv_sem=erecv_sem.at[k],
            device_id={"line": lax.rem(me + k, LINES)},
            device_id_type=MESH,
        )

    @pl.loop(1, LINES)
    def _(k):
        share(k).start()

    for c in range(2):

        @pl.loop(0, LINES)
        def _(k, c=c):
            onward(c, k).wait_send()

        @pl.loop(1, LINES)
        def _(k, c=c):
            direct(c, k).wait_send()

    erecv[0] = energy

    @pl.loop(1, LINES)
    def _(k):
        share(k).wait_recv()

    total = jnp.sum(jnp.sum(erecv[...], axis=0), axis=(0, 1), keepdims=True)
    scale = lax.rsqrt(total / (RKEEP * AZ) + 1e-06)

    @pl.loop(0, ROWS)
    def _(r):
        for comp in range(2):
            v = img[pl.ds(pl.multiple_of(64 * r + 32 * comp, 32), 32), :]
            out_ref[comp, r] = (v * scale).astype(BF16)

    @pl.loop(1, LINES)
    def _(k):
        share(k).wait_send()


def local(echoes, range_filter, rcmc_weights, fm_rate, rcmc_shift, seam_width, seam_link):
    import functools

    weights = rcmc_weights.reshape(TAPS, 128, 32).transpose(0, 2, 1)
    vmem = pl.BlockSpec(memory_space=pltpu.VMEM)
    smem = pl.BlockSpec(memory_space=pltpu.SMEM)
    hbm = pl.BlockSpec(memory_space=pl.ANY)
    dma = pltpu.SemaphoreType.DMA
    image = pl.pallas_call(
        functools.partial(kernel, lax.axis_size("chip")),
        out_shape=jax.ShapeDtypeStruct((2, ROWS, 32, 128), BF16),
        in_specs=[hbm, vmem, vmem, smem, smem, smem, smem] + [vmem] * 8,
        out_specs=vmem,
        scratch_shapes=[
            pltpu.VMEM((2, 256, 4096), BF16),
            pltpu.VMEM((64, 128), F32),
            pltpu.VMEM((80, 128), F32),
            pltpu.VMEM((4, 34 * 128, 128), BF16),
            pltpu.VMEM((RKEEP, 256), F32),
            pltpu.VMEM((2, 48 * LINES, 128), F32),
            pltpu.VMEM((2 * LINES * SLOT, 128), F32),
            pltpu.VMEM((32 * NEED, 256), BF16),
            pltpu.VMEM((32 * NEED, 256), BF16),
            pltpu.VMEM((NEED, 32, 256), F32),
            pltpu.VMEM((ROWS, 32, 128), F32),
            pltpu.VMEM((ROWS, 32, 128), F32),
            pltpu.VMEM((32 * ROWS, 256), BF16),
            pltpu.VMEM((32 * ROWS, 256), BF16),
            pltpu.VMEM((32 * ROWS, 256), F32),
            pltpu.VMEM((64 * ROWS, 128), F32),
            pltpu.VMEM((2 * ROWS, 128), F32),
            pltpu.VMEM((2 * ROWS, 128), F32),
            pltpu.VMEM((8, 128), F32),
            pltpu.VMEM((LINES, 8, 128), F32),
            dma((2,)),
            dma((2, LINES)),
            dma((2, LINES)),
            dma((2, LINES)),
            dma((2, LINES)),
            dma((2,)),
            dma((LINES,)),
            dma((LINES,)),
        ],
        compiler_params=pltpu.CompilerParams(
            collective_id=0, has_side_effects=True, vmem_limit_bytes=48 * 1024 * 1024
        ),
        name="focus",
    )(
        echoes,
        range_filter,
        weights,
        fm_rate,
        rcmc_shift,
        seam_width,
        seam_link,
        *(jnp.asarray(t) for t in tables()),
    )
    return image.reshape(1, 2, ROWS, AZ)


def solution(mesh):
    in_specs = (
        P("chip", None, "line", None),
        P(),
        P(),
        P("chip", "line"),
        P("chip", "line"),
        P("chip"),
        P("chip"),
    )
    out_specs = P("chip", None, "line", None)
    return jax.shard_map(local, mesh=mesh, in_specs=in_specs, out_specs=out_specs, check_vma=False)
```

profile of v0, /device:TPU:2, one launch (start us, length us, event | category | flops | bytes accessed | tf_op | source)
XLA Modules:
  0.0 82.2 jit_solution(9133236492959577397)
XLA Ops:
  1.3 1.1 %reshape.6 = f32[8,128,32]{2,1,0:T(8,128)S(1)} reshape(f32[8,4096]{1,0:T(8,128)} %param.17) | data formatting | bytes 262144 | tf_op jit(solution)/shard_map/reshape | solution.py:451
  2.4 0.2 copy.16
  2.5 0.0 copy-start
  2.5 2.2 %copy-done = bf16[1,2,256,4096]{3,2,1,0:T(8,128)(2,1)S(1)} copy-done((bf16[1,2,256,4096]{3,2,1,0:T(8,128)(2,1)S(1)}, bf16[1,2,256,4096]{3,2,1,0:T(8,128)(2,1)}, u32[]{:S(2)}) %copy-start) | copy-done | bytes 4194328
  4.7 0.0 copy-start.1
  4.7 1.0 %copy-done.1 = bf16[768,256]{1,0:T(8,128)(2,1)S(1)} copy-done((bf16[768,256]{1,0:T(8,128)(2,1)S(1)}, bf16[768,256]{1,0:T(8,128)(2,1)}, u32[]{:S(2)}) %copy-start.1) | copy-done | bytes 393240
  5.7 0.0 copy-start.2
  5.7 1.0 %copy-done.2 = bf16[768,256]{1,0:T(8,128)(2,1)S(1)} copy-done((bf16[768,256]{1,0:T(8,128)(2,1)S(1)}, bf16[768,256]{1,0:T(8,128)(2,1)}, u32[]{:S(2)}) %copy-start.2) | copy-done | bytes 393240
  6.7 0.0 copy-start.3
  6.7 0.9 %copy-done.3 = f32[256,256]{1,0:T(8,128)S(1)} copy-done((f32[256,256]{1,0:T(8,128)S(1)}, f32[256,256]{1,0:T(8,128)}, u32[]{:S(2)}) %copy-start.3) | copy-done | bytes 262168
  7.7 0.0 copy-start.4
  7.7 0.8 copy-done.4
  8.4 0.0 copy-start.5
  8.4 0.8 copy-done.5
  9.2 0.0 copy-start.6
  9.2 0.8 copy-done.6
  10.0 0.0 copy-start.7
  10.0 0.8 copy-done.7
  10.7 0.0 copy-start.8
  10.7 0.8 copy-done.8
  11.5 0.0 copy-start.9
  11.5 0.7 copy-done.9
  12.1 0.0 copy-start.10
  12.1 0.7 copy-done.10
  12.8 68.5 %focus.1 = bf16[2,24,32,128]{3,2,1,0:T(8,128)(2,1)S(1)} custom-call(bf16[1,2,256,4096]{3,2,1,0:T(8,128)(2,1)S(1)} %copy-done, f32[2,4096]{1,0:T(2,128)S(1)} %copy-done.5, f32[8,32,128]{2,1,0:T(8,128)S(1)} %bitcast.3, f32[1,24]{1,0:T(1,128)S(1)} %copy-done.9, s32[1,24]{1,0:T(1,128)S(1)} %copy-done.10, s32[1]{0:T(128)S(6)} %copy.17.width_ref, ...), custom_call_target="tpu_custom_call" | custom-call | tf_op jit(solution)/shard_map/focus/pallas_call | solution.py:456
  81.3 0.9 %reshape.7 = bf16[1,2,24,4096]{3,2,1,0:T(8,128)(2,1)} reshape(bf16[2,24,32,128]{3,2,1,0:T(8,128)(2,1)S(1)} %focus.1) | data formatting | bytes 786432 | tf_op jit(solution)/shard_map/reshape | solution.py:505
Async XLA Ops:
  2.5 2.2 %copy-start = (bf16[1,2,256,4096]{3,2,1,0:T(8,128)(2,1)S(1)}, bf16[1,2,256,4096]{3,2,1,0:T(8,128)(2,1)}, u32[]{:S(2)}) copy-start(bf16[1,2,256,4096]{3,2,1,0:T(8,128)(2,1)} %echo_hbm.1) | copy-start | bytes 12582916
  4.7 1.0 %copy-start.1 = (bf16[768,256]{1,0:T(8,128)(2,1)S(1)}, bf16[768,256]{1,0:T(8,128)(2,1)}, u32[]{:S(2)}) copy-start(bf16[768,256]{1,0:T(8,128)(2,1)} %constant.19.clone.inv128_ref) | copy-start | bytes 1179652
  5.7 1.0 %copy-start.2 = (bf16[768,256]{1,0:T(8,128)(2,1)S(1)}, bf16[768,256]{1,0:T(8,128)(2,1)}, u32[]{:S(2)}) copy-start(bf16[768,256]{1,0:T(8,128)(2,1)} %constant.18.clone.fwd128_ref) | copy-start | bytes 1179652
  6.7 0.9 %copy-start.3 = (f32[256,256]{1,0:T(8,128)S(1)}, f32[256,256]{1,0:T(8,128)}, u32[]{:S(2)}) copy-start(f32[256,256]{1,0:T(8,128)} %constant.16.clone.second_ref) | copy-start | bytes 786436
  7.7 0.8 copy-start.4
  8.4 0.8 copy-start.5
  9.2 0.8 copy-start.6
  10.0 0.8 copy-start.7
  10.7 0.8 copy-start.8
  11.5 0.7 copy-start.9
  12.1 0.7 copy-start.10
where the time goes:
time: 82.9 us; the launch traced here: 82.2 us
  Pallas kernels  68.5 us (83%)
  local copies, waits for them, and re-layouts  12.4 us (15%)
  between operations  1.33 us (2%)
    pallas_call x1, Pallas kernels, local(): pl.pallas_call(functools.partial(kernel, lax.axis_size('chip')), out_shap...  68.5 us
    unnamed x22, local copies, waits for them, and re-layouts  10.2 us

commit v1 on v0

--- a/solution.py
+++ b/solution.py
@@ -98,12 +98,25 @@
 def kernel(
     chips,
     echo_hbm,
+    filter_hbm,
+    weight_hbm,
+    rate_hbm,
+    shift_hbm,
+    width_ref,
+    link_ref,
+    first_hbm,
+    fturn_hbm,
+    second_hbm,
+    fwd32_hbm,
+    turn_hbm,
+    fwd128_hbm,
+    inv128_hbm,
+    inv32_hbm,
+    out_ref,
     filter_ref,
     weight_ref,
     rate_ref,
     shift_ref,
-    width_ref,
-    link_ref,
     first_ref,
     fturn_ref,
     second_ref,
@@ -112,7 +125,6 @@
     fwd128_ref,
     inv128_ref,
     inv32_ref,
-    out_ref,
     echo,
     spectrum,
     pulse,
@@ -120,6 +132,8 @@
     acc,
     piece,
     recv,
+    gathered,
+    weights,
     mid_hi,
     mid_lo,
     ext,
@@ -133,11 +147,13 @@
     tail_in,
     esend,
     erecv,
+    table_sem,
     load_sem,
     send_sem,
     recv_sem,
+    hsend_sem,
+    hrecv_sem,
     fsend_sem,
-    frecv_sem,
     tail_sem,
     esend_sem,
     erecv_sem,
@@ -146,7 +162,6 @@
     chip = lax.axis_index("chip")
     following = lax.rem(chip + 1, chips)
     preceding = lax.rem(chip + chips - 1, chips)
-    below = lax.rem(me + LINES - 1, LINES)
     barrier = pltpu.get_barrier_semaphore()
 
     @pl.loop(1, LINES)
@@ -165,8 +180,33 @@
             load_sem.at[c],
         )
 
+    pairs = (
+        (filter_hbm, filter_ref),
+        (first_hbm, first_ref),
+        (fturn_hbm, fturn_ref),
+        (second_hbm, second_ref),
+        (rate_hbm, rate_ref),
+        (shift_hbm, shift_ref),
+        (weight_hbm, weight_ref),
+        (fwd32_hbm, fwd32_ref),
+        (turn_hbm, turn_ref),
+        (fwd128_hbm, fwd128_ref),
+        (inv128_hbm, inv128_ref),
+        (inv32_hbm, inv32_ref),
+    )
+    fetch = [
+        pltpu.make_async_copy(a, b, table_sem.at[i]) for i, (a, b) in enumerate(pairs)
+    ]
+    for copy in fetch[:4]:
+        copy.start()
     load(0).start()
     load(1).start()
+    for copy in fetch[4:]:
+        copy.start()
+    for c in range(2):
+        piece[c, pl.ds(48 * LINES, 40), :] = jnp.zeros((40, 128), F32)
+    for copy in fetch[:4]:
+        copy.wait()
 
     for comp in range(2):
         for a in range(32):
@@ -202,31 +242,28 @@
             new.append(ahead)
         return tuple(new)
 
-    lax.fori_loop(0, 34, build, (slanted(0, 0), slanted(1, 0)))
-
-    def multiply(c):
-        acc[...] = jnp.zeros_like(acc)
-
-        @pl.loop(0, 16)
-        def _(t):
-            s = pl.multiple_of(256 * t, 256)
-            at0 = pl.multiple_of(128 * lax.rem(32 - 2 * t, 32), 128)
-            at1 = pl.multiple_of(128 * (31 - 2 * t), 128)
-            xr = echo[0, 128 * c : 128 * c + 128, pl.ds(s, 256)]
-            xi = echo[1, 128 * c : 128 * c + 128, pl.ds(s, 256)]
-            right = jnp.concatenate(
-                [
-                    jnp.concatenate([xr, xr, -xi, -xi], axis=1),
-                    jnp.concatenate([xi, xi, xr, xr], axis=1),
-                ],
-                axis=0,
-            )
-            left = jnp.concatenate(
-                [band[part, pl.ds(at, RKEEP), :] for part in range(4) for at in (at0, at1)],
-                axis=1,
-            )
-            acc[...] += mm_nt(left, right)
-
+    def step(c, t, at0, at1):
+        s = pl.multiple_of(256 * t, 256)
+        xr = echo[0, 128 * c : 128 * c + 128, pl.ds(s, 256)]
+        xi = echo[1, 128 * c : 128 * c + 128, pl.ds(s, 256)]
+        right = jnp.concatenate(
+            [
+                jnp.concatenate([xr, xr, -xi, -xi], axis=1),
+                jnp.concatenate([xi, xi, xr, xr], axis=1),
+            ],
+            axis=0,
+        )
+        left = jnp.concatenate(
+            [
+                band[part, pl.ds(pl.multiple_of(128 * at, 128), RKEEP), :]
+                for part in range(4)
+                for at in (at0, at1)
+            ],
+            axis=1,
+        )
+        acc[...] += mm_nt(left, right)
+
+    def pack(c):
         for g in range(LINES):
             ramp = lax.broadcasted_iota(jnp.int32, (ROWS, 1), 0) + ROWS * g
             gain = 1.0 + 2.0 * ramp.astype(F32) / RKEEP
@@ -237,43 +274,119 @@
                 piece[c, base + 32 + 4 * comp : base + 36 + 4 * comp, :] = v[16:20]
                 piece[c, base + 40 + 4 * comp : base + 44 + 4 * comp, :] = v[20:]
 
+    acc[...] = jnp.zeros_like(acc)
+    carry = lax.fori_loop(0, 5, build, (slanted(0, 0), slanted(1, 0)))
+    load(0).wait()
+
+    def first_pass(i, carry):
+        carry = build(2 * i + 6, build(2 * i + 5, carry))
+        step(0, 15 - i, 2 * i + 2, 2 * i + 1)
+        return carry
+
+    lax.fori_loop(0, 15, first_pass, carry)
+    step(0, 0, 0, 31)
+    pack(0)
+
+    odd = lax.rem(me, 2) == 1
+
+    def order(j):
+        return jnp.where(lax.rem(j, 2) == 0, 15 - j // 2, (j + 1) // 2)
+
+    def slot_of(source, c):
+        return (2 * source + c) * SLOT
+
     def direct(c, k):
         to = lax.rem(me + k, LINES)
         return pltpu.make_async_remote_copy(
             src_ref=piece.at[c, pl.ds(pl.multiple_of(48 * to, 8), 48), :],
-            dst_ref=recv.at[pl.ds(pl.multiple_of((2 * me + c) * SLOT, 8), 48), :],
+            dst_ref=recv.at[pl.ds(pl.multiple_of(slot_of(me, c), 8), 48), :],
             send_sem=send_sem.at[c, k],
             recv_sem=recv_sem.at[c, k],
             device_id={"line": to},
             device_id_type=MESH,
         )
 
+    def margin(c, k):
+        to = lax.rem(me + k, LINES)
+        return pltpu.make_async_remote_copy(
+            src_ref=piece.at[c, pl.ds(pl.multiple_of(48 * to + 48, 8), 40), :],
+            dst_ref=recv.at[pl.ds(pl.multiple_of(slot_of(me, c) + 48, 8), 40), :],
+            send_sem=hsend_sem.at[c, k],
+            recv_sem=hrecv_sem.at[c, k],
+            device_id={"line": to},
+            device_id_type=MESH,
+        )
+
     def onward(c, k):
-        source = lax.rem(me + LINES - k, LINES)
-        slot = (2 * source + c) * SLOT
+        slot = slot_of(lax.rem(me + LINES - k, LINES), c)
         return pltpu.make_async_remote_copy(
             src_ref=recv.at[pl.ds(pl.multiple_of(slot, 8), 40), :],
             dst_ref=recv.at[pl.ds(pl.multiple_of(slot + 48, 8), 40), :],
             send_sem=fsend_sem.at[c, k],
-            recv_sem=frecv_sem.at[c, k],
-            device_id={"line": below},
+            recv_sem=hrecv_sem.at[c, k],
+            device_id={"line": lax.rem(me + LINES - 1, LINES)},
             device_id_type=MESH,
         )
 
-    for c in range(2):
-        load(c).wait()
-        multiply(c)
-        if c == 0:
-            pl.semaphore_wait(barrier, LINES + 1)
-
-        @pl.loop(1, LINES)
-        def _(k, c=c):
+    def to_odd(k):
+        return lax.rem(me + k, 2) == 1
+
+    def send(c):
+        @pl.loop(0, LINES - 1)
+        def _(j):
+            k = order(j)
             direct(c, k).start()
 
-        recv[pl.ds(pl.multiple_of((2 * me + c) * SLOT, 8), 48), :] = piece[
-            c, pl.ds(pl.multiple_of(48 * me, 8), 48), :
-        ]
-        onward(c, 0).start()
+            @pl.when(to_odd(k))
+            def _():
+                margin(c, k).start()
+
+        own = pl.multiple_of(48 * me, 8)
+        at = pl.multiple_of(slot_of(me, c), 8)
+        recv[pl.ds(at, 48), :] = piece[c, pl.ds(own, 48), :]
+
+        @pl.when(odd)
+        def _():
+            recv[pl.ds(at + 48, 40), :] = piece[c, pl.ds(pl.multiple_of(own + 48, 8), 40), :]
+            onward(c, 0).start()
+
+    def hand_on(c):
+        @pl.loop(0, LINES - 1)
+        def _(j):
+            k = order(j)
+            direct(c, k).wait_recv()
+
+            @pl.when(odd)
+            def _():
+                onward(c, k).start()
+
+    pl.semaphore_wait(barrier, LINES + 1)
+    send(0)
+    acc[...] = jnp.zeros_like(acc)
+    load(1).wait()
+
+    @pl.loop(0, 16)
+    def _(t):
+        step(1, t, lax.rem(32 - 2 * t, 32), 31 - 2 * t)
+
+    pack(1)
+    send(1)
+    for copy in fetch[4:]:
+        copy.wait()
+    hand_on(0)
+
+    for a in range(32):
+        gathered[8 * a : 8 * a + 8, :] = weight_ref[:, 128 * a : 128 * a + 128]
+    row = lax.broadcasted_iota(jnp.int32, (128, 128), 0)
+    target = 4 * lax.rem(row, 32) + row // 32
+    spread = (lax.broadcasted_iota(jnp.int32, (128, 128), 1) == target).astype(F32).astype(BF16)
+    spread = jnp.concatenate([spread, spread, spread], axis=0)
+    for t in range(TAPS):
+        v = gathered[pl.ds(t, 32, stride=8), :].T
+        v = jnp.concatenate([v[32 * u : 32 * u + 32] for u in range(4)], axis=1)
+        high = v.astype(BF16)
+        middle, low = split(v - high.astype(F32))
+        weights[t] = mm(jnp.concatenate([high, middle, low], axis=1), spread)
 
     index = lax.broadcasted_iota(jnp.int32, (32, 128), 0) + 32 * lax.broadcasted_iota(
         jnp.int32, (32, 128), 1
@@ -288,38 +401,41 @@
         cosine[r] = jnp.cos(math.pi * turns)
         sine[r] = jnp.sin(math.pi * turns)
 
-    for c in range(2):
-
-        @pl.loop(1, LINES)
-        def _(k, c=c):
-            direct(c, k).wait_recv()
-            onward(c, k).start()
-
-    for c in range(2):
-
-        @pl.loop(0, LINES)
-        def _(k, c=c):
-            onward(c, k).wait_recv()
+    hand_on(1)
 
     tc, ts = turn_ref[0], turn_ref[1]
-    last = me == LINES - 1
 
     def column(i):
         def part(comp):
             at = place(comp, i) if i < ROWS else 48 + place(comp, i - ROWS)
             return recv[pl.ds(at, 32, stride=SLOT), :]
 
-        v = jnp.concatenate([part(0), part(1)], axis=0)
-        return v if i < ROWS else jnp.where(last, 0.0, v)
-
-    for i in range(0, NEED, 2):
-        high, low = split(jnp.concatenate([column(i), column(i + 1)], axis=1))
-        y = mm(fwd32_ref[...], jnp.concatenate([high, low, high], axis=0))
-        for j in range(2):
-            yr, yi = turned(y[:32, 128 * j : 128 * j + 128], y[32:, 128 * j : 128 * j + 128], tc, ts)
-            high, low = split(jnp.concatenate([yr, yi], axis=1))
-            mid_hi[32 * (i + j) : 32 * (i + j) + 32, :] = high
-            mid_lo[32 * (i + j) : 32 * (i + j) + 32, :] = low
+        return jnp.concatenate([part(0), part(1)], axis=0)
+
+    def across(first, last):
+        for i in range(first, last, 2):
+            high, low = split(jnp.concatenate([column(i), column(i + 1)], axis=1))
+            y = mm(fwd32_ref[...], jnp.concatenate([high, low, high], axis=0))
+            for j in range(2):
+                yr, yi = turned(
+                    y[:32, 128 * j : 128 * j + 128], y[32:, 128 * j : 128 * j + 128], tc, ts
+                )
+                high_j, low_j = split(jnp.concatenate([yr, yi], axis=1))
+                mid_hi[32 * (i + j) : 32 * (i + j) + 32, :] = high_j
+                mid_lo[32 * (i + j) : 32 * (i + j) + 32, :] = low_j
+
+    across(0, ROWS)
+    for c in range(2):
+
+        @pl.loop(0, LINES - 1)
+        def _(j, c=c):
+            margin(c, order(j)).wait_recv()
+
+        @pl.when(jnp.logical_not(odd))
+        def _(c=c):
+            margin(c, 0).wait_recv()
+
+    across(ROWS, NEED)
 
     @pl.loop(0, 4)
     def _(j):
@@ -334,7 +450,7 @@
         real = jnp.zeros((32, 128), F32)
         imag = jnp.zeros((32, 128), F32)
         for t in range(TAPS):
-            w = weight_ref[t]
+            w = weights[t]
             row = ext[at + t]
             real += w * row[:, :128]
             imag += w * row[:, 128:]
@@ -417,13 +533,19 @@
 
     for c in range(2):
 
-        @pl.loop(0, LINES)
-        def _(k, c=c):
-            onward(c, k).wait_send()
-
         @pl.loop(1, LINES)
         def _(k, c=c):
             direct(c, k).wait_send()
+
+            @pl.when(to_odd(k))
+            def _():
+                margin(c, k).wait_send()
+
+        @pl.when(odd)
+        def _(c=c):
+            @pl.loop(0, LINES)
+            def _(k):
+                onward(c, k).wait_send()
 
     erecv[0] = energy
 
@@ -448,24 +570,37 @@
 def local(echoes, range_filter, rcmc_weights, fm_rate, rcmc_shift, seam_width, seam_link):
     import functools
 
-    weights = rcmc_weights.reshape(TAPS, 128, 32).transpose(0, 2, 1)
     vmem = pl.BlockSpec(memory_space=pltpu.VMEM)
     smem = pl.BlockSpec(memory_space=pltpu.SMEM)
-    hbm = pl.BlockSpec(memory_space=pl.ANY)
+    hbm = pl.BlockSpec(memory_space=pltpu.HBM)
     dma = pltpu.SemaphoreType.DMA
     image = pl.pallas_call(
         functools.partial(kernel, lax.axis_size("chip")),
         out_shape=jax.ShapeDtypeStruct((2, ROWS, 32, 128), BF16),
-        in_specs=[hbm, vmem, vmem, smem, smem, smem, smem] + [vmem] * 8,
+        in_specs=[hbm] * 5 + [smem] * 2 + [hbm] * 8,
         out_specs=vmem,
         scratch_shapes=[
+            pltpu.VMEM((2, 4096), F32),
+            pltpu.VMEM((TAPS, 4096), F32),
+            pltpu.SMEM((1, ROWS), F32),
+            pltpu.SMEM((1, ROWS), jnp.int32),
+            pltpu.VMEM((64, 64), F32),
+            pltpu.VMEM((2, 32, 128), F32),
+            pltpu.VMEM((256, 256), F32),
+            pltpu.VMEM((64, 192), BF16),
+            pltpu.VMEM((2, 32, 128), F32),
+            pltpu.VMEM((768, 256), BF16),
+            pltpu.VMEM((768, 256), BF16),
+            pltpu.VMEM((64, 192), BF16),
             pltpu.VMEM((2, 256, 4096), BF16),
             pltpu.VMEM((64, 128), F32),
             pltpu.VMEM((80, 128), F32),
-            pltpu.VMEM((4, 34 * 128, 128), BF16),
+            pltpu.VMEM((4, 35 * 128, 128), BF16),
             pltpu.VMEM((RKEEP, 256), F32),
-            pltpu.VMEM((2, 48 * LINES, 128), F32),
+            pltpu.VMEM((2, 48 * LINES + 40, 128), F32),
             pltpu.VMEM((2 * LINES * SLOT, 128), F32),
+            pltpu.VMEM((32 * TAPS, 128), F32),
+            pltpu.VMEM((TAPS, 32, 128), F32),
             pltpu.VMEM((32 * NEED, 256), BF16),
             pltpu.VMEM((32 * NEED, 256), BF16),
             pltpu.VMEM((NEED, 32, 256), F32),
@@ -479,7 +614,9 @@
             pltpu.VMEM((2 * ROWS, 128), F32),
             pltpu.VMEM((8, 128), F32),
             pltpu.VMEM((LINES, 8, 128), F32),
+            dma((12,)),
             dma((2,)),
+            dma((2, LINES)),
             dma((2, LINES)),
             dma((2, LINES)),
             dma((2, LINES)),
@@ -489,13 +626,13 @@
             dma((LINES,)),
         ],
         compiler_params=pltpu.CompilerParams(
-            collective_id=0, has_side_effects=True, vmem_limit_bytes=48 * 1024 * 1024
+            collective_id=0, has_side_effects=True, vmem_limit_bytes=67_043_328
         ),
         name="focus",
     )(
         echoes,
         range_filter,
-        weights,
+        rcmc_weights,
         fm_rate,
         rcmc_shift,
         seam_width,

time: 82.9 us -> 66.4 us (0.80)
  local copies, waits for them, and re-layouts: 12.4 us -> 1.91 us
  Pallas kernels: 68.5 us -> 63 us
    unnamed x22 -> x0, local copies, waits for them, and re-layouts: 10.2 us -> none
    pallas_call x1, Pallas kernels: 68.5 us -> 63 us  [local(): pl.pallas_call(functools.partial(kernel, lax.axis_size('chip')), out_shap...]
    reshape x2 -> x0, local copies, waits for them, and re-layouts: 1.24 us -> none  [local(): weights = rcmc_weights.reshape(TAPS, 128, 32).transpose(0, 2, 1)]
    reshape x1, local copies, waits for them, and re-layouts: 0.91 us -> 1.91 us  [local(): return image.reshape(1, 2, ROWS, AZ)]
where the time goes in v1:
time: 66.4 us; the launch traced here: 66.2 us
  Pallas kernels  63 us (95%)
  local copies, waits for them, and re-layouts  1.91 us (3%)
  between operations  1.3 us (2%)
    pallas_call x1, Pallas kernels, local(): pl.pallas_call(functools.partial(kernel, lax.axis_size('chip')), out_shap...  63 us
    reshape x1, local copies, waits for them, and re-layouts, local(): return image.reshape(1, 2, ROWS, AZ)  1.91 us

profile of v1, /device:TPU:2, one launch (start us, length us, event | category | flops | bytes accessed | tf_op | source)
XLA Modules:
  0.0 66.2 jit_solution(4634972383534989371)
XLA Ops:
  1.3 63.0 %focus.1 = bf16[2,24,32,128]{3,2,1,0:T(8,128)(2,1)} custom-call(bf16[1,2,256,4096]{3,2,1,0:T(8,128)(2,1)} %echo_hbm.1, f32[2,4096]{1,0:T(2,128)} %filter_hbm.1, f32[8,4096]{1,0:T(8,128)} %weight_hbm.1, f32[1,24]{1,0:T(1,128)} %rate_hbm.1, s32[1,24]{1,0:T(1,128)} %shift_hbm.1, s32[1]{0:T(128)S(6)} %copy.16.width_ref, s32[1]{0:T(128)S(6)} %copy.17.link_ref, ...), custom_call_target="tpu_custom_call" | custom-call | tf_op jit(solution)/shard_map/focus/pallas_call | solution.py:577
  64.3 1.9 %reshape.3 = bf16[1,2,24,4096]{3,2,1,0:T(8,128)(2,1)} reshape(bf16[2,24,32,128]{3,2,1,0:T(8,128)(2,1)} %focus.1) | data formatting | bytes 786432 | tf_op jit(solution)/shard_map/reshape | solution.py:642

commit v2 on v1

--- a/solution.py
+++ b/solution.py
@@ -17,6 +17,7 @@
 LINES = 16
 ROWS = RKEEP // LINES
 NEED = 44
+PITCH = 72
 SLOT = 104
 HIGHEST = lax.Precision.HIGHEST
 MESH = pl.DeviceIdType.MESH
@@ -66,6 +67,8 @@
     inverse128 = np.block([[c, s], [-s, c]])
     c, s = angles(n32, n32, 32, 1)
     inverse32 = np.block([[c, -s], [s, c]]) / 4096.0
+    ends = np.concatenate([inverse32[31::32], np.zeros((14, 64))])
+    inverse32 = np.concatenate([inverse32, ends])
     f32 = lambda t: t.astype(np.float32)
     return (
         f32(first),
@@ -242,7 +245,19 @@
             new.append(ahead)
         return tuple(new)
 
-    def step(c, t, at0, at1):
+    def window(part, at, half):
+        at = 128 * at
+        if half is None:
+            return band[part, pl.ds(pl.multiple_of(at, 128), RKEEP), :]
+        return jnp.concatenate(
+            [
+                band[part, pl.ds(pl.multiple_of(at + 96 * j + 48 * half, 16), 48), :]
+                for j in range(4)
+            ],
+            axis=0,
+        )
+
+    def step(c, t, at0, at1, half=None):
         s = pl.multiple_of(256 * t, 256)
         xr = echo[0, 128 * c : 128 * c + 128, pl.ds(s, 256)]
         xi = echo[1, 128 * c : 128 * c + 128, pl.ds(s, 256)]
@@ -254,28 +269,40 @@
             axis=0,
         )
         left = jnp.concatenate(
-            [
-                band[part, pl.ds(pl.multiple_of(128 * at, 128), RKEEP), :]
-                for part in range(4)
-                for at in (at0, at1)
-            ],
-            axis=1,
-        )
-        acc[...] += mm_nt(left, right)
-
-    def pack(c):
+            [window(part, at, half) for part in range(4) for at in (at0, at1)], axis=1
+        )
+        acc[: left.shape[0], :] += mm_nt(left, right)
+
+    def pack(c, half=None):
         for g in range(LINES):
+            if half is not None and g // 2 % 2 != half:
+                continue
+            row = ROWS * g if half is None else 48 * (g // 4) + ROWS * (g % 2)
             ramp = lax.broadcasted_iota(jnp.int32, (ROWS, 1), 0) + ROWS * g
             gain = 1.0 + 2.0 * ramp.astype(F32) / RKEEP
             for comp in range(2):
-                v = acc[ROWS * g : ROWS * g + ROWS, 128 * comp : 128 * comp + 128] * gain
+                v = acc[row : row + ROWS, 128 * comp : 128 * comp + 128] * gain
                 base = 48 * g
                 piece[c, base + 16 * comp : base + 16 * comp + 16, :] = v[:16]
                 piece[c, base + 32 + 4 * comp : base + 36 + 4 * comp, :] = v[16:20]
                 piece[c, base + 40 + 4 * comp : base + 44 + 4 * comp, :] = v[20:]
 
-    acc[...] = jnp.zeros_like(acc)
-    carry = lax.fori_loop(0, 5, build, (slanted(0, 0), slanted(1, 0)))
+    def clear():
+        acc[...] = jnp.zeros_like(acc)
+
+    def sweep(c, half=None):
+        clear()
+
+        @pl.loop(0, 16)
+        def _(t):
+            step(c, t, lax.rem(32 - 2 * t, 32), 31 - 2 * t, half)
+
+        pack(c, half)
+
+    clear()
+    carry = (slanted(0, 0), slanted(1, 0))
+    for m in range(5):
+        carry = build(m, carry)
     load(0).wait()
 
     def first_pass(i, carry):
@@ -328,19 +355,22 @@
             device_id_type=MESH,
         )
 
-    def to_odd(k):
-        return lax.rem(me + k, 2) == 1
-
-    def send(c):
+    def each(action):
         @pl.loop(0, LINES - 1)
         def _(j):
             k = order(j)
+            action(k, lax.rem(me + k, LINES))
+
+    def start_direct(c, k, to, half=None):
+        if half is None:
             direct(c, k).start()
-
-            @pl.when(to_odd(k))
-            def _():
-                margin(c, k).start()
-
+        else:
+            pl.when(lax.rem(to // 2, 2) == half)(lambda: direct(c, k).start())
+
+    def start_margin(c, k, to):
+        pl.when(lax.rem(to, 2) == 1)(lambda: margin(c, k).start())
+
+    def keep_own(c):
         own = pl.multiple_of(48 * me, 8)
         at = pl.multiple_of(slot_of(me, c), 8)
         recv[pl.ds(at, 48), :] = piece[c, pl.ds(own, 48), :]
@@ -350,31 +380,30 @@
             recv[pl.ds(at + 48, 40), :] = piece[c, pl.ds(pl.multiple_of(own + 48, 8), 40), :]
             onward(c, 0).start()
 
-    def hand_on(c):
-        @pl.loop(0, LINES - 1)
-        def _(j):
-            k = order(j)
-            direct(c, k).wait_recv()
-
-            @pl.when(odd)
-            def _():
-                onward(c, k).start()
+    def hand_on(c, k):
+        direct(c, k).wait_recv()
+        pl.when(odd)(lambda: onward(c, k).start())
 
     pl.semaphore_wait(barrier, LINES + 1)
-    send(0)
-    acc[...] = jnp.zeros_like(acc)
+
+    def second(k, to):
+        start_direct(0, k, to)
+        start_margin(0, k, to)
+
+    each(second)
+    keep_own(0)
     load(1).wait()
-
-    @pl.loop(0, 16)
-    def _(t):
-        step(1, t, lax.rem(32 - 2 * t, 32), 31 - 2 * t)
-
-    pack(1)
-    send(1)
+    sweep(1)
     for copy in fetch[4:]:
         copy.wait()
-    hand_on(0)
-
+
+    def third(k, to):
+        hand_on(0, k)
+        start_direct(1, k, to)
+        start_margin(1, k, to)
+
+    each(third)
+    keep_own(1)
     for a in range(32):
         gathered[8 * a : 8 * a + 8, :] = weight_ref[:, 128 * a : 128 * a + 128]
     row = lax.broadcasted_iota(jnp.int32, (128, 128), 0)
@@ -401,7 +430,7 @@
         cosine[r] = jnp.cos(math.pi * turns)
         sine[r] = jnp.sin(math.pi * turns)
 
-    hand_on(1)
+    each(lambda k, to: hand_on(1, k))
 
     tc, ts = turn_ref[0], turn_ref[1]
 
@@ -424,7 +453,17 @@
                 mid_hi[32 * (i + j) : 32 * (i + j) + 32, :] = high_j
                 mid_lo[32 * (i + j) : 32 * (i + j) + 32, :] = low_j
 
+    def along(first, count):
+        @pl.loop(0, 2)
+        def _(j):
+            row = first + count // 2 * j
+            at = pl.ds(pl.multiple_of(32 * row, 32), 16 * count)
+            high, low = mid_hi[at, :], mid_lo[at, :]
+            y = mm(jnp.concatenate([high, low, high], axis=1), fwd128_ref[...])
+            ext[pl.ds(row, count // 2)] = y.reshape(count // 2, 32, 256)
+
     across(0, ROWS)
+    along(0, ROWS)
     for c in range(2):
 
         @pl.loop(0, LINES - 1)
@@ -436,15 +475,9 @@
             margin(c, 0).wait_recv()
 
     across(ROWS, NEED)
-
-    @pl.loop(0, 4)
-    def _(j):
-        at = pl.multiple_of(352 * j, 32)
-        high, low = mid_hi[pl.ds(at, 352), :], mid_lo[pl.ds(at, 352), :]
-        y = mm(jnp.concatenate([high, low, high], axis=1), fwd128_ref[...])
-        ext[pl.ds(11 * j, 11)] = y.reshape(11, 32, 256)
-
-    @pl.loop(0, ROWS)
+    along(ROWS, NEED - ROWS)
+
+    @pl.loop(0, ROWS, unroll=2)
     def _(r):
         at = r + shift_ref[0, r]
         real = jnp.zeros((32, 128), F32)
@@ -472,12 +505,14 @@
             vr, vi = turned(v[:, :128], v[:, 128:], tc, -ts)
             both.append(jnp.concatenate([vr, vi], axis=0))
         high, low = split(jnp.concatenate(both, axis=1))
-        y = mm(inv32_ref[...], jnp.concatenate([high, low, high], axis=0))
+        foc_hi[32 * i : 32 * i + 64, :] = high
+        foc_lo[32 * i : 32 * i + 64, :] = low
+        y = mm(inv32_ref[64:80, :], jnp.concatenate([high, low, high], axis=0))
         for j in range(2):
-            img[64 * (i + j) : 64 * (i + j) + 64, :] = y[:, 128 * j : 128 * j + 128]
-
-    for comp in range(2):
-        tail[ROWS * comp : ROWS * comp + ROWS, :] = img[pl.ds(32 * comp + 31, ROWS, stride=64), :]
+            for comp in range(2):
+                row = ROWS * comp + i + j
+                tail[row : row + 1, :] = y[comp : comp + 1, 128 * j : 128 * j + 128]
+
     handed = pltpu.make_async_remote_copy(
         src_ref=tail,
         dst_ref=tail_in,
@@ -488,10 +523,16 @@
     )
     handed.start()
 
+    for i in range(0, ROWS, 2):
+        high, low = foc_hi[32 * i : 32 * i + 64, :], foc_lo[32 * i : 32 * i + 64, :]
+        y = mm(inv32_ref[:64, :], jnp.concatenate([high, low, high], axis=0))
+        for j in range(2):
+            img[PITCH * (i + j) : PITCH * (i + j) + 64, :] = y[:, 128 * j : 128 * j + 128]
+
     rest = (lax.broadcasted_iota(jnp.int32, (8, 128), 0) > 0).astype(F32)
 
     def gather(r, total):
-        v = img[pl.ds(pl.multiple_of(64 * r, 64), 64), :]
+        v = img[pl.ds(pl.multiple_of(PITCH * r, 8), 64), :]
         v = v * v
         for j in range(8):
             part = v[8 * j : 8 * j + 8]
@@ -509,10 +550,10 @@
     earlier = jnp.where(chip == 0, 0.0, tail_in[...])
     previous = pltpu.roll(earlier, lax.rem(width, OVL), axis=1)
     for comp in range(2):
-        head = img[pl.ds(32 * comp, ROWS, stride=64), :]
+        head = img[pl.ds(32 * comp, ROWS, stride=PITCH), :]
         before = previous[ROWS * comp : ROWS * comp + ROWS]
         mixed = jnp.where(inside, (1.0 - ramp) * before + ramp * head, head)
-        img[pl.ds(32 * comp, ROWS, stride=64), :] = mixed
+        img[pl.ds(32 * comp, ROWS, stride=PITCH), :] = mixed
         mixed = mixed * mixed
         energy = energy + mixed[:8] + mixed[8:16] + mixed[16:]
     esend[...] = energy
@@ -537,7 +578,7 @@
         def _(k, c=c):
             direct(c, k).wait_send()
 
-            @pl.when(to_odd(k))
+            @pl.when(lax.rem(me + k, 2) == 1)
             def _():
                 margin(c, k).wait_send()
 
@@ -556,11 +597,12 @@
     total = jnp.sum(jnp.sum(erecv[...], axis=0), axis=(0, 1), keepdims=True)
     scale = lax.rsqrt(total / (RKEEP * AZ) + 1e-06)
 
-    @pl.loop(0, ROWS)
-    def _(r):
+    @pl.loop(0, 32)
+    def _(m):
         for comp in range(2):
-            v = img[pl.ds(pl.multiple_of(64 * r + 32 * comp, 32), 32), :]
-            out_ref[comp, r] = (v * scale).astype(BF16)
+            v = img[pl.ds(32 * comp + m, ROWS, stride=PITCH), :]
+            at = pl.ds(pl.multiple_of(128 * m, 128), 128)
+            out_ref[0, comp, :, at] = (v * scale).astype(BF16)
 
     @pl.loop(1, LINES)
     def _(k):
@@ -576,7 +618,7 @@
     dma = pltpu.SemaphoreType.DMA
     image = pl.pallas_call(
         functools.partial(kernel, lax.axis_size("chip")),
-        out_shape=jax.ShapeDtypeStruct((2, ROWS, 32, 128), BF16),
+        out_shape=jax.ShapeDtypeStruct((1, 2, ROWS, AZ), BF16),
         in_specs=[hbm] * 5 + [smem] * 2 + [hbm] * 8,
         out_specs=vmem,
         scratch_shapes=[
@@ -591,7 +633,7 @@
             pltpu.VMEM((2, 32, 128), F32),
             pltpu.VMEM((768, 256), BF16),
             pltpu.VMEM((768, 256), BF16),
-            pltpu.VMEM((64, 192), BF16),
+            pltpu.VMEM((80, 192), BF16),
             pltpu.VMEM((2, 256, 4096), BF16),
             pltpu.VMEM((64, 128), F32),
             pltpu.VMEM((80, 128), F32),
@@ -609,7 +651,7 @@
             pltpu.VMEM((32 * ROWS, 256), BF16),
             pltpu.VMEM((32 * ROWS, 256), BF16),
             pltpu.VMEM((32 * ROWS, 256), F32),
-            pltpu.VMEM((64 * ROWS, 128), F32),
+            pltpu.VMEM((PITCH * ROWS, 128), F32),
             pltpu.VMEM((2 * ROWS, 128), F32),
             pltpu.VMEM((2 * ROWS, 128), F32),
             pltpu.VMEM((8, 128), F32),
@@ -639,7 +681,7 @@
         seam_link,
         *(jnp.asarray(t) for t in tables()),
     )
-    return image.reshape(1, 2, ROWS, AZ)
+    return image
 
 
 def solution(mesh):

time: 66.4 us -> 65.5 us (0.986)
  Pallas kernels: 63 us -> 62.2 us
    reshape x1 -> x0, local copies, waits for them, and re-layouts: 1.91 us -> none  [local(): return image.reshape(1, 2, ROWS, AZ)]
    unnamed x0 -> x1, local copies, waits for them, and re-layouts: none -> 1.77 us
    pallas_call x1, Pallas kernels: 63 us -> 62.2 us  [local(): pl.pallas_call(functools.partial(kernel, lax.axis_size('chip')), out_shap...]
where the time goes in v2:
time: 65.5 us; the launch traced here: 65.3 us
  Pallas kernels  62.2 us (95%)
  local copies, waits for them, and re-layouts  1.77 us (3%)
  between operations  1.3 us (2%)
    pallas_call x1, Pallas kernels, local(): pl.pallas_call(functools.partial(kernel, lax.axis_size('chip')), out_shap...  62.2 us
    unnamed x1, local copies, waits for them, and re-layouts  1.77 us

profile of v2, /device:TPU:2, one launch (start us, length us, event | category | flops | bytes accessed | tf_op | source)
XLA Modules:
  0.0 65.3 jit_solution(15303475118981928527)
XLA Ops:
  1.3 62.2 %focus.1 = bf16[1,2,24,4096]{3,2,1,0:T(8,128)(2,1)} custom-call(bf16[1,2,256,4096]{3,2,1,0:T(8,128)(2,1)} %echo_hbm.1, f32[2,4096]{1,0:T(2,128)} %filter_hbm.1, f32[8,4096]{1,0:T(8,128)} %weight_hbm.1, f32[1,24]{1,0:T(1,128)} %rate_hbm.1, s32[1,24]{1,0:T(1,128)} %shift_hbm.1, s32[1]{0:T(128)S(6)} %copy.17.width_ref, s32[1]{0:T(128)S(6)} %copy.18.link_ref, ...), custom_call_target="tpu_custom_call" | custom-call | tf_op jit(solution)/shard_map/focus/pallas_call | solution.py:619
  63.5 1.8 %copy.19 = bf16[1,2,24,4096]{3,2,1,0:T(8,128)(2,1)} copy(bf16[1,2,24,4096]{3,2,1,0:T(8,128)(2,1)} %focus.1) | data formatting | bytes 786432

commit v3 on v2

--- a/solution.py
+++ b/solution.py
@@ -245,39 +245,27 @@
             new.append(ahead)
         return tuple(new)
 
-    def window(part, at, half):
-        at = 128 * at
-        if half is None:
-            return band[part, pl.ds(pl.multiple_of(at, 128), RKEEP), :]
-        return jnp.concatenate(
-            [
-                band[part, pl.ds(pl.multiple_of(at + 96 * j + 48 * half, 16), 48), :]
-                for j in range(4)
-            ],
-            axis=0,
-        )
-
-    def step(c, t, at0, at1, half=None):
-        s = pl.multiple_of(256 * t, 256)
-        xr = echo[0, 128 * c : 128 * c + 128, pl.ds(s, 256)]
-        xi = echo[1, 128 * c : 128 * c + 128, pl.ds(s, 256)]
+    def step(c, tiles):
+        left, upper, lower = [], [], []
+        for t, at0, at1 in tiles:
+            s = pl.ds(pl.multiple_of(256 * t, 256), 256)
+            xr = echo[0, 128 * c : 128 * c + 128, s]
+            xi = echo[1, 128 * c : 128 * c + 128, s]
+            upper += [xr, xr, -xi, -xi]
+            lower += [xi, xi, xr, xr]
+            left += [
+                band[part, pl.ds(pl.multiple_of(128 * at, 128), RKEEP), :]
+                for part in range(4)
+                for at in (at0, at1)
+            ]
         right = jnp.concatenate(
-            [
-                jnp.concatenate([xr, xr, -xi, -xi], axis=1),
-                jnp.concatenate([xi, xi, xr, xr], axis=1),
-            ],
-            axis=0,
-        )
-        left = jnp.concatenate(
-            [window(part, at, half) for part in range(4) for at in (at0, at1)], axis=1
-        )
-        acc[: left.shape[0], :] += mm_nt(left, right)
-
-    def pack(c, half=None):
+            [jnp.concatenate(upper, axis=1), jnp.concatenate(lower, axis=1)], axis=0
+        )
+        acc[...] += mm_nt(jnp.concatenate(left, axis=1), right)
+
+    def pack(c):
         for g in range(LINES):
-            if half is not None and g // 2 % 2 != half:
-                continue
-            row = ROWS * g if half is None else 48 * (g // 4) + ROWS * (g % 2)
+            row = ROWS * g
             ramp = lax.broadcasted_iota(jnp.int32, (ROWS, 1), 0) + ROWS * g
             gain = 1.0 + 2.0 * ramp.astype(F32) / RKEEP
             for comp in range(2):
@@ -290,28 +278,34 @@
     def clear():
         acc[...] = jnp.zeros_like(acc)
 
-    def sweep(c, half=None):
+    def sweep(c):
         clear()
 
-        @pl.loop(0, 16)
-        def _(t):
-            step(c, t, lax.rem(32 - 2 * t, 32), 31 - 2 * t, half)
-
-        pack(c, half)
+        @pl.loop(0, 8)
+        def _(p):
+            t = 2 * p
+            step(
+                c,
+                [(t, lax.rem(32 - 2 * t, 32), 31 - 2 * t), (t + 1, 30 - 2 * t, 29 - 2 * t)],
+            )
+
+        pack(c)
 
     clear()
     carry = (slanted(0, 0), slanted(1, 0))
-    for m in range(5):
+    for m in range(7):
         carry = build(m, carry)
     load(0).wait()
 
-    def first_pass(i, carry):
-        carry = build(2 * i + 6, build(2 * i + 5, carry))
-        step(0, 15 - i, 2 * i + 2, 2 * i + 1)
+    def first_pass(p, carry):
+        for m in range(4):
+            carry = build(4 * p + 7 + m, carry)
+        t = 15 - 2 * p
+        step(0, [(t, 4 * p + 2, 4 * p + 1), (t - 1, 4 * p + 4, 4 * p + 3)])
         return carry
 
-    lax.fori_loop(0, 15, first_pass, carry)
-    step(0, 0, 0, 31)
+    lax.fori_loop(0, 7, first_pass, carry)
+    step(0, [(1, 30, 29), (0, 0, 31)])
     pack(0)
 
     odd = lax.rem(me, 2) == 1
@@ -361,12 +355,6 @@
             k = order(j)
             action(k, lax.rem(me + k, LINES))
 
-    def start_direct(c, k, to, half=None):
-        if half is None:
-            direct(c, k).start()
-        else:
-            pl.when(lax.rem(to // 2, 2) == half)(lambda: direct(c, k).start())
-
     def start_margin(c, k, to):
         pl.when(lax.rem(to, 2) == 1)(lambda: margin(c, k).start())
 
@@ -387,7 +375,7 @@
     pl.semaphore_wait(barrier, LINES + 1)
 
     def second(k, to):
-        start_direct(0, k, to)
+        direct(0, k).start()
         start_margin(0, k, to)
 
     each(second)
@@ -399,7 +387,7 @@
 
     def third(k, to):
         hand_on(0, k)
-        start_direct(1, k, to)
+        direct(1, k).start()
         start_margin(1, k, to)
 
     each(third)

time: 65.5 us -> 63.8 us (0.974)
  Pallas kernels: 62.2 us -> 60.5 us
    pallas_call x1, Pallas kernels: 62.2 us -> 60.5 us  [local(): pl.pallas_call(functools.partial(kernel, lax.axis_size('chip')), out_shap...]
where the time goes in v3:
time: 63.8 us; the launch traced here: 63.6 us
  Pallas kernels  60.5 us (95%)
  local copies, waits for them, and re-layouts  1.77 us (3%)
  between operations  1.3 us (2%)
    pallas_call x1, Pallas kernels, local(): pl.pallas_call(functools.partial(kernel, lax.axis_size('chip')), out_shap...  60.5 us
    unnamed x1, local copies, waits for them, and re-layouts  1.77 us

profile of v3, /device:TPU:2, one launch (start us, length us, event | category | flops | bytes accessed | tf_op | source)
XLA Modules:
  0.0 63.6 jit_solution(14519542475569595573)
XLA Ops:
  1.3 60.5 %focus.1 = bf16[1,2,24,4096]{3,2,1,0:T(8,128)(2,1)} custom-call(bf16[1,2,256,4096]{3,2,1,0:T(8,128)(2,1)} %echo_hbm.1, f32[2,4096]{1,0:T(2,128)} %filter_hbm.1, f32[8,4096]{1,0:T(8,128)} %weight_hbm.1, f32[1,24]{1,0:T(1,128)} %rate_hbm.1, s32[1,24]{1,0:T(1,128)} %shift_hbm.1, s32[1]{0:T(128)S(6)} %copy.17.width_ref, s32[1]{0:T(128)S(6)} %copy.18.link_ref, ...), custom_call_target="tpu_custom_call" | custom-call | tf_op jit(solution)/shard_map/focus/pallas_call | solution.py:607
  61.8 1.8 %copy.19 = bf16[1,2,24,4096]{3,2,1,0:T(8,128)(2,1)} copy(bf16[1,2,24,4096]{3,2,1,0:T(8,128)(2,1)} %focus.1) | data formatting | bytes 786432
